TPU v7x, 32 devices: a 4x4x1 block of a 4x4x8 slice. The times are simulated.
32 devices in a mesh: dp: 1 (over z), tp: 32 (over x, y, core).
Axes of the slice: x: 4, y: 4, z: 1, core: 2. Of those that a mesh axis runs over, the one named last changes fastest.
The devices are a block of a 4x4x8 slice.
Arguments:
- x: bfloat16 [2048, 5120], P('dp')
- dy: bfloat16 [2048, 5120], P('dp')
- gate: bfloat16 [2048, 12288], P('dp', 'tp')
- up: bfloat16 [2048, 12288], P('dp', 'tp')
- w_gate: bfloat16 [5120, 12288], P(None, 'tp')
- w_up: bfloat16 [5120, 12288], P(None, 'tp')
- w_down: bfloat16 [12288, 5120], P('tp')
Outputs:
- output 1: bfloat16 [2048, 5120], P('dp')
- output 2: bfloat16 [5120, 12288], P('dp', 'tp')
- output 3: bfloat16 [5120, 12288], P('dp', 'tp')
- output 4: bfloat16 [12288, 5120], P(('dp', 'tp'))
All inputs are finite; a program needn't handle non-finite values.
Results may differ from a plain program's by a relative error of at most 0.012.
Values are sent between devices in bfloat16 or wider.
A program may use at most 768 MiB of HBM per device.

v0:
```python
import jax
import jax.numpy as jnp
from jax import lax
from jax.sharding import PartitionSpec as P


def act(gate, up):
    return jax.nn.silu(gate) * up


def solution(mesh):
    def step(x, dy, gate, up, w_gate, w_up, w_down):
        hidden, back = jax.vjp(act, gate.astype(jnp.float32), up.astype(jnp.float32))
        d_hidden = jnp.dot(dy, w_down.T, preferred_element_type=jnp.float32)
        d_gate, d_up = (g.astype(jnp.bfloat16) for g in back(d_hidden))
        term = jnp.dot(d_gate, w_gate.T, preferred_element_type=jnp.float32) + jnp.dot(d_up, w_up.T, preferred_element_type=jnp.float32)
        dx = lax.psum(term.astype(jnp.bfloat16), "tp")
        dw_gate = jnp.dot(x.T, d_gate, preferred_element_type=jnp.float32)
        dw_up = jnp.dot(x.T, d_up, preferred_element_type=jnp.float32)
        dw_down = jnp.dot(hidden.astype(jnp.bfloat16).T, dy, preferred_element_type=jnp.float32)
        return dx, *(g.astype(jnp.bfloat16) for g in (dw_gate, dw_up, dw_down))

    tokens, columns, rows = P("dp", None), P(None, "tp"), P("tp", None)
    return jax.shard_map(
        step,
        mesh=mesh,
        in_specs=(tokens, tokens, P("dp", "tp"), P("dp", "tp"), columns, columns, rows),
        out_specs=(tokens, P("dp", "tp"), P("dp", "tp"), P(("dp", "tp"), None)),
        check_vma=False,
    )
```

profile of v0, /device:TPU:97, one launch (start us, length us, event | category | flops | bytes accessed | tf_op | source)
XLA Modules:
  0.0 275.1 jit_solution(3496754501643384349)
XLA Ops:
  7.2 0.1 all-reduce.2.cloned.1.call-start
  7.2 18.6 %fusion.8 = (bf16[2048,384]{1,0:T(8,128)(2,1)}, f32[2048,384]{1,0:T(8,128)S(1)}) fusion(bf16[2048,384]{1,0:T(8,128)(2,1)} %param.9, bf16[2048,384]{1,0:T(8,128)(2,1)} %param.10, bf16[2048,5120]{1,0:T(8,128)(2,1)} %param.8, bf16[384,5120]{1,0:T(8,128)(2,1)} %param.13), kind=kOutput, calls=%fused_computation.18 | convolution fusion | flops 8063287296 | bytes 32768000 | tf_op jit(solution)/shard_map/dot_general | solution.py:14
  25.9 0.0 copy-start
  25.9 21.2 %fusion.11 = f32[2048,5120]{1,0:T(8,128)} fusion(bf16[2048,384]{1,0:T(8,128)(2,1)} %get-tuple-element.8, bf16[5120,384]{1,0:T(8,128)(2,1)} %param.11), kind=kOutput, calls=%fused_computation.21 | convolution fusion | flops 8053063680 | bytes 47448064 | tf_op jit(solution)/shard_map/dot_general | solution.py:16
  47.1 0.0 copy-done
  47.1 24.1 %add_convert_fusion = bf16[2048,5120]{1,0:T(8,128)(2,1)} fusion(f32[2048,5120]{1,0:T(8,128)} %fusion.11, bf16[5120,384]{1,0:T(8,128)(2,1)} %param.12, f32[2048,384]{1,0:T(8,128)S(1)} %get-tuple-element.9, bf16[2048,384]{1,0:T(8,128)(2,1)S(1)} %copy-done), kind=kOutput, calls=%fused_computation | convolution fusion | flops 8079540224 | bytes 71565312 | tf_op jit(solution)/shard_map/dot_general | solution.py:16
  71.2 0.1 all-reduce.2.cloned.1.call-update
  71.2 14.5 %fusion = bf16[5120,384]{0,1:T(8,128)(2,1)} fusion(bf16[2048,384]{1,0:T(8,128)(2,1)} %get-tuple-element.8, bf16[2048,5120]{1,0:T(8,128)(2,1)} %param.7), kind=kOutput, calls=%fused_computation.4 | convolution fusion | flops 8055029760 | bytes 26476544 | tf_op jit(solution)/shard_map/dot_general | solution.py:18
  85.7 6.3 %copy.11 = bf16[5120,384]{1,0:T(8,128)(2,1)} copy(bf16[5120,384]{0,1:T(8,128)(2,1)} %fusion) | data formatting | bytes 7864320
  91.9 14.6 %fusion.1 = bf16[5120,384]{0,1:T(8,128)(2,1)} fusion(bf16[2048,5120]{1,0:T(8,128)(2,1)} %param.7, f32[2048,384]{1,0:T(8,128)S(1)} %get-tuple-element.9, bf16[2048,384]{1,0:T(8,128)(2,1)} %param.9), kind=kOutput, calls=%fused_computation.5 | convolution fusion | flops 8060534784 | bytes 29622272 | tf_op jit(solution)/shard_map/dot_general | solution.py:19
  106.6 0.0 copy-start.1
  106.6 0.0 copy-start.2
  106.6 6.4 %copy.12 = bf16[5120,384]{1,0:T(8,128)(2,1)} copy(bf16[5120,384]{0,1:T(8,128)(2,1)} %fusion.1) | data formatting | bytes 7864320
  113.0 0.0 copy-done.1
  113.0 0.0 copy-done.2
  113.0 14.7 %convolution_convert_fusion = bf16[384,5120]{1,0:T(8,128)(2,1)} fusion(bf16[2048,5120]{1,0:T(8,128)(2,1)} %param.8, bf16[2048,384]{1,0:T(8,128)(2,1)S(1)} %copy-done.2, bf16[2048,384]{1,0:T(8,128)(2,1)S(1)} %copy-done.1), kind=kOutput, calls=%fused_computation.1 | convolution fusion | flops 8061321216 | bytes 28049408 | tf_op jit(solution)/shard_map/dot_general | solution.py:20
  127.7 123.3 %all-reduce.2.cloned.1.call-done = bf16[2048,5120]{1,0:T(8,128)(2,1)} async-done(((bf16[2048,5120]{1,0:T(8,128)(2,1)}), bf16[2048,5120]{1,0:T(8,128)(2,1)}) %all-reduce.2.cloned.1.call-update) | async-done | bytes 20971536 | tf_op jit(solution)/shard_map/psum | solution.py:17
  250.9 17.3 %copy.14 = bf16[2048,5120]{1,0:T(8,128)(2,1)} copy(bf16[2048,5120]{1,0:T(8,128)(2,1)} %all-reduce.2.cloned.1.call-done) | data formatting | bytes 41943040
Async XLA Ops:
  7.2 243.8 %all-reduce.2.cloned.1.call-start = ((), (), s32[]{:S(2)}) async-start(), calls=%async_computation | async-start | bytes 41943040 | tf_op jit(solution)/shard_map/psum | solution.py:17
  25.9 21.2 %copy-start = (bf16[2048,384]{1,0:T(8,128)(2,1)S(1)}, bf16[2048,384]{1,0:T(8,128)(2,1)}, u32[]{:S(2)}) copy-start(bf16[2048,384]{1,0:T(8,128)(2,1)} %param.9) | copy-start | bytes 4718596
  106.6 6.4 %copy-start.1 = (bf16[2048,384]{1,0:T(8,128)(2,1)S(1)}, bf16[2048,384]{1,0:T(8,128)(2,1)}, u32[]{:S(2)}) copy-start(bf16[2048,384]{1,0:T(8,128)(2,1)} %param.9) | copy-start | bytes 4718596
  106.6 6.4 %copy-start.2 = (bf16[2048,384]{1,0:T(8,128)(2,1)S(1)}, bf16[2048,384]{1,0:T(8,128)(2,1)}, u32[]{:S(2)}) copy-start(bf16[2048,384]{1,0:T(8,128)(2,1)} %param.10) | copy-start | bytes 4718596
Sparse Core Ops, SparseCore 0:
  71.3 179.5 all-reduce.1
where the time goes:
time: 276 us; the launch traced here: 275 us
  waiting for transfers between devices  123 us (45%)
  matrix products  108 us (39%)
  local copies, waits for them, and re-layouts  30 us (11%)
  between operations  14.1 us (5%)
    psum x1, waiting for transfers between devices, step(): dx = lax.psum(term.astype(jnp.bfloat16), 'tp')  123 us
    unnamed x9, local copies, waits for them, and re-layouts  30 us
    dot_general x1, matrix products, step(): jnp.dot(d_up, w_up.T, preferred_element_type=jnp.float32)  24.1 us
    dot_general x1, matrix products, step(): jnp.dot(d_gate, w_gate.T, preferred_element_type=jnp.float32)  21.2 us
    dot_general x1, matrix products, step(): d_hidden = jnp.dot(dy, w_down.T, preferred_element_type=jnp.float32)  18.6 us
    dot_general x1, matrix products, step(): jnp.dot(hidden.astype(jnp.bfloat16).T, dy, preferred_element_type=jnp.flo...  14.7 us
    dot_general x1, matrix products, step(): dw_up = jnp.dot(x.T, d_up, preferred_element_type=jnp.float32)  14.6 us
    dot_general x1, matrix products, step(): dw_gate = jnp.dot(x.T, d_gate, preferred_element_type=jnp.float32)  14.5 us
  transfers between devices with their start and end apart: 1, of which 1 were waited for; matrix products, arithmetic and copies ran while one was open for 21% of the time, Pallas kernels for 0%

commit v1 on v0

v1 whole, which is shorter than its diff:
```python
import functools
import math

import jax
import jax.numpy as jnp
from jax import lax
from jax.experimental import pallas as pl
from jax.experimental.pallas import tpu as pltpu
from jax.sharding import PartitionSpec as P

MESH = pl.DeviceIdType.MESH
HALF = 256
SLOTS = 3
COLS = 256
F32, BF16 = jnp.float32, jnp.bfloat16
NT = (((1,), (1,)), ((), ()))
TN = (((0,), (0,)), ((), ()))
NN = (((1,), (0,)), ((), ()))


def dot(a, b, dims):
    return lax.dot_general(a, b, dims, preferred_element_type=F32)


def kernel(
    n, x, dy, gate, up, w_gate, w_up, w_down,
    dx, dw_gate, dw_up, dw_down,
    wd, wgu, dgu, hid, sums, outbox, dy_rows, g_rows, u_rows, x_cols, dy_cols, st_gu, st_d,
    ring_send, ring_recv, pair_send, pair_recv, credit, w_sem, row_sem, col_sem, out_sem,
):
    rows, width = x.shape
    ff = gate.shape[1]
    chunks = rows // (2 * HALF)
    block = width // n
    sub = HALF // n
    hr, hc = HALF // 2, block // 2
    units = width // COLS

    me = lax.axis_index("tp")
    c = lax.rem(me, 2)
    chip = me // 2
    px, py = chip // n, lax.rem(chip, n)
    p1 = px * (1 - c) + py * c
    p2 = py * (1 - c) + px * c

    def device(ax, ay, core):
        return (lax.rem(ax, n) * n + lax.rem(ay, n)) * 2 + core

    sx, sy = 1 - c, c
    right1, left1 = device(px + sx, py + sy, c), device(px + n - sx, py + n - sy, c)
    right2, left2 = device(px + sy, py + sx, c), device(px + n - sy, py + n - sx, c)
    partner = device(px, py, 1 - c)
    q1 = px * c + py * (1 - c)

    def mod(v):
        return lax.rem(v + n, n)

    def own(k):
        return pl.multiple_of((2 * k + c) * HALF, HALF)

    def other(k):
        return pl.multiple_of((2 * k + 1 - c) * HALF, HALF)

    def cols(b):
        return pl.multiple_of(b * block, 128)

    def remote(src, dst, ssem, rsem, to):
        return pltpu.make_async_remote_copy(
            src_ref=src, dst_ref=dst, send_sem=ssem, recv_sem=rsem, device_id={"tp": to}, device_id_type=MESH
        )

    def rs1_src(k, b, h):
        return sums.at[lax.rem(k, SLOTS), b, pl.ds(h * hr, hr), :]

    def rs1_land(k, area, h):
        return dx.at[pl.ds(other(k) + h * hr, hr), pl.ds(area * block, block)]

    def rs2_src(k, s, h):
        return sums.at[lax.rem(k, SLOTS), p1, pl.ds(pl.multiple_of(s * sub, sub), sub), pl.ds(h * hc, hc)]

    def rs2_land(k, area, h):
        return dx.at[pl.ds(other(k) + area * sub, sub), pl.ds(3 * block + h * hc, hc)]

    def ag2_at(k, s, h):
        return dx.at[pl.ds(own(k) + pl.multiple_of(s * sub, sub), sub), pl.ds(cols(p1) + h * hc, hc)]

    def ag1_at(k, b, h):
        return dx.at[pl.ds(own(k) + h * hr, hr), pl.ds(cols(b), block)]

    land = {0: (0, 0), 1: (0, 1), 2: (1, 1), 3: (2, 0), 4: (1, 0), 5: (2, 1)}

    def reduce_pair(src, dst, p, i):
        which = {0: (2, 0), 1: (2, 1), 2: (n - 1, 1), 3: (1, 0), 4: (n - 1, 0), 5: (1, 1)}[i]
        return src(mod(p + which[0]), which[1]), dst(*land[i])

    def gather_at(at, p, i, arriving):
        off, h = {0: (0, 0), 1: (0, 1), 2: (0, 1), 3: (0, 0), 4: (1, 0), 5: (n - 1, 1)}[i]
        step = (1 if i % 2 == 0 else n - 1) if arriving else 0
        return at(mod(p + off + step), h)

    def ring(phase, k, i, arriving=False):
        left, right = (left1, right1) if phase in (0, 3) else (left2, right2)
        if phase == 0:
            src, dst = reduce_pair(functools.partial(rs1_src, k), functools.partial(rs1_land, k), p1, i)
        elif phase == 1:
            src, dst = reduce_pair(functools.partial(rs2_src, k), functools.partial(rs2_land, k), p2, i)
        elif phase == 2:
            src = dst = gather_at(functools.partial(ag2_at, k), p2, i, arriving)
        else:
            src = dst = gather_at(functools.partial(ag1_at, k), p1, i, arriving)
        to = left if i % 2 == 0 else right
        return remote(src, dst, ring_send.at[k, phase, i], ring_recv.at[k, phase, i], to)

    def send(phase, k, *which):
        for i in which:
            ring(phase, k, i).start()

    def arrive(phase, k, *which):
        for i in which:
            ring(phase, k, i, arriving=True).wait_recv()

    def reduced(k):
        for phase in (0, 1):
            for i in range(6):
                ring(phase, k, i).wait_send()

    def swap(k, o):
        b = lax.rem(q1 + 2 + o, n)
        return remote(
            outbox.at[o], dx.at[pl.ds(other(k), HALF), pl.ds(cols(b), block)],
            pair_send.at[k, o], pair_recv.at[k, o], partner,
        )

    def swap_in(k, o):
        b = lax.rem(p1 + 2 + o, n)
        return remote(
            outbox.at[o], dx.at[pl.ds(own(k), HALF), pl.ds(cols(b), block)],
            pair_send.at[k, o], pair_recv.at[k, o], partner,
        )

    def share(k, i):
        b = mod(p1 + (0, 1, n - 1, 2)[i])
        at = dx.at[pl.ds(own(k), HALF), pl.ds(cols(b), block)]
        return remote(at, at, pair_send.at[k, 4 + i], pair_recv.at[k, 4 + i], partner)

    def share_in(k, i):
        b = mod(q1 + (0, 1, n - 1, 2)[i])
        at = dx.at[pl.ds(other(k), HALF), pl.ds(cols(b), block)]
        return remote(at, at, pair_send.at[k, 4 + i], pair_recv.at[k, 4 + i], partner)

    def row_copies(b):
        at = pl.ds(pl.multiple_of((2 * (b // 2) + lax.rem(b + 1 + c, 2)) * HALF, HALF), HALF)
        slot = lax.rem(b, 2)
        return [
            pltpu.make_async_copy(src.at[at, :], dst.at[slot], row_sem.at[slot, i])
            for i, (src, dst) in enumerate(((dy, dy_rows), (gate, g_rows), (up, u_rows)))
        ]

    def col_copies(u):
        at = pl.ds(pl.multiple_of(u * COLS, COLS), COLS)
        slot = lax.rem(u, 2)
        return [
            pltpu.make_async_copy(src.at[:, at], dst.at[slot], col_sem.at[slot, i])
            for i, (src, dst) in enumerate(((x, x_cols), (dy, dy_cols)))
        ]

    def out_copies(u):
        at = pl.ds(pl.multiple_of(u * COLS, COLS), COLS)
        slot = lax.rem(u, 2)
        return [
            pltpu.make_async_copy(st_gu.at[slot, :, pl.ds(0, ff)], dw_gate.at[at, :], out_sem.at[slot, 0]),
            pltpu.make_async_copy(st_gu.at[slot, :, pl.ds(ff, ff)], dw_up.at[at, :], out_sem.at[slot, 1]),
            pltpu.make_async_copy(st_d.at[slot], dw_down.at[:, at], out_sem.at[slot, 2]),
        ]

    load_wd = pltpu.make_async_copy(w_down, wd, w_sem.at[0])
    load_wg = pltpu.make_async_copy(w_gate, wgu.at[:, pl.ds(0, ff)], w_sem.at[1])
    load_wu = pltpu.make_async_copy(w_up, wgu.at[:, pl.ds(ff, ff)], w_sem.at[2])

    def hidden_grads(b):
        for copy in row_copies(b):
            copy.wait()
        slot = lax.rem(b, 2)
        at = pl.multiple_of((2 * (b // 2) + lax.rem(b + 1 + c, 2)) * HALF, HALF)
        d_hidden = dot(dy_rows[slot], wd[...], NT)
        g, u = g_rows[slot].astype(F32), u_rows[slot].astype(F32)
        sig = jax.nn.sigmoid(g)
        silu = g * sig
        dgu[pl.ds(at, HALF), pl.ds(0, ff)] = (d_hidden * u * (sig + silu * (1.0 - sig))).astype(BF16)
        dgu[pl.ds(at, HALF), pl.ds(ff, ff)] = (d_hidden * silu).astype(BF16)
        hid[:, pl.ds(at, HALF)] = (silu * u).T.astype(BF16)

        @pl.when(b + 2 < 2 * chunks)
        def _():
            for copy in row_copies(b + 2):
                copy.start()

    def term(at, b):
        return dot(dgu[pl.ds(at, HALF), :], wgu[pl.ds(pl.multiple_of(b * block, 128), block), :], NT)

    def partner_half(k):
        hidden_grads(2 * k)

        @pl.when(k == 0)
        def _():
            load_wg.wait()
            load_wu.wait()

        @pl.loop(0, n)
        def _(o):
            @pl.when(k > 0)
            def _():
                swap(k - 1, o).wait_send()

            outbox[o] = term(other(k), lax.rem(q1 + 2 + o, n)).astype(BF16)
            swap(k, o).start()

    def own_half(k):
        hidden_grads(2 * k + 1)
        pl.when(k >= SLOTS)(lambda: reduced(k - SLOTS))

        @pl.loop(0, n)
        def _(o):
            b = lax.rem(p1 + 2 + o, n)
            t = term(own(k), b)
            swap_in(k, o).wait_recv()
            sums[lax.rem(k, SLOTS), b] = (t + dx[pl.ds(own(k), HALF), pl.ds(cols(b), block)].astype(F32)).astype(BF16)

            @pl.when(o == 0)
            def _():
                send(0, k, 0, 1)

            @pl.when(o == 1)
            def _():
                send(0, k, 2)

            @pl.when(o == 3)
            def _():
                send(0, k, 3)

    def weight_grads(u):
        for copy in col_copies(u):
            copy.wait()
        slot = lax.rem(u, 2)

        @pl.when(u >= 2)
        def _():
            for copy in out_copies(u - 2):
                copy.wait()

        st_gu[slot] = dot(x_cols[slot], dgu[...], TN).astype(BF16)
        st_d[slot] = dot(hid[...], dy_cols[slot], NN).astype(BF16)
        for copy in out_copies(u):
            copy.start()

        @pl.when(u + 2 < units)
        def _():
            for copy in col_copies(u + 2):
                copy.start()

    def add(dst, size, *srcs):
        step = 32

        @pl.loop(0, size // step)
        def _(r):
            at = pl.multiple_of(r * step, step)
            total = srcs[0](at, step).astype(F32)
            for s in srcs[1:]:
                total = total + s(at, step).astype(F32)
            dst(at, step, total.astype(BF16))

    def add_sums(k, b, off, size, lanes, *lands):
        def mine(at, step):
            return sums[lax.rem(k, SLOTS), b, pl.ds(off + at, step), lanes]

        def put(at, step, v):
            sums[lax.rem(k, SLOTS), b, pl.ds(off + at, step), lanes] = v

        add(put, size, mine, *lands)

    def landed(row, first, wide):
        return lambda at, step: dx[pl.ds(row + at, step), pl.ds(first, wide)]

    def s1(k):
        arrive(0, k, 0)
        add_sums(k, mod(p1 + n - 1), 0, hr, slice(None), landed(other(k), 0, block))
        send(0, k, 4)
        arrive(0, k, 1)
        add_sums(k, mod(p1 + 1), hr, hr, slice(None), landed(other(k) + hr, 0, block))
        send(0, k, 5)

    def s2(k):
        arrive(0, k, 2, 3, 4, 5)
        add_sums(k, p1, 0, HALF, slice(None), landed(other(k), block, block), landed(other(k), 2 * block, block))
        send(1, k, 0, 1, 2, 3)

    def s3(k):
        base = 3 * block
        arrive(1, k, 0)
        add_sums(k, p1, pl.multiple_of(mod(p2 + n - 1) * sub, sub), sub, pl.ds(0, hc), landed(other(k), base, hc))
        send(1, k, 4)
        arrive(1, k, 1)
        add_sums(k, p1, pl.multiple_of(mod(p2 + 1) * sub, sub), sub, pl.ds(hc, hc), landed(other(k), base + hc, hc))
        send(1, k, 5)

    def s4(k):
        arrive(1, k, 2, 3, 4, 5)
        off = pl.multiple_of(p2 * sub, sub)

        def put(at, step, v):
            dx[pl.ds(own(k) + off + at, step), pl.ds(cols(p1), block)] = v

        add(
            put, sub,
            lambda at, step: sums[lax.rem(k, SLOTS), p1, pl.ds(off + at, step), :],
            landed(other(k) + sub, 3 * block, block),
            landed(other(k) + 2 * sub, 3 * block, block),
        )
        send(2, k, 0, 1, 2, 3)
        pl.semaphore_signal(credit.at[k], inc=1, device_id={"tp": partner}, device_id_type=MESH)

    def s5(k):
        arrive(2, k, 0)
        send(2, k, 4)
        arrive(2, k, 1)
        send(2, k, 5)

    def s6(k):
        arrive(2, k, 2, 3, 4, 5)
        send(3, k, 0, 1, 2, 3)
        pl.semaphore_wait(credit.at[k], 1)
        share(k, 0).start()

    def s7(k):
        arrive(3, k, 0)
        send(3, k, 4)
        arrive(3, k, 1)
        send(3, k, 5)

    def s8(k):
        arrive(3, k, 2)
        share(k, 1).start()
        arrive(3, k, 3)
        share(k, 2).start()
        arrive(3, k, 4, 5)
        share(k, 3).start()

    def s9(k):
        for i in range(n):
            share_in(k, i).wait_recv()

    def at_chunk(stage, k):
        pl.when(jnp.logical_and(k >= 0, k < chunks))(lambda: stage(k))

    def some_units(slot):
        @pl.loop(0, 4)
        def _(i):
            u = slot * 4 + i
            pl.when(u < units)(lambda: weight_grads(u))

    load_wd.start()
    for b in range(2):
        for copy in row_copies(b):
            copy.start()
    load_wg.start()
    load_wu.start()
    barrier = pltpu.get_barrier_semaphore()
    for to in (left1, right1, left2, right2, partner):
        pl.semaphore_signal(barrier, inc=1, device_id={"tp": to}, device_id_type=MESH)
    pl.semaphore_wait(barrier, 5)
    load_wd.wait()

    @pl.loop(0, chunks + 5)
    def _(j):
        late = j >= chunks
        pl.when(j < chunks)(lambda: partner_half(j))
        pl.when(late)(lambda: some_units(2 * (j - chunks)))
        at_chunk(s1, j - 1)
        at_chunk(s3, j - 2)
        at_chunk(s5, j - 3)
        at_chunk(s7, j - 4)
        at_chunk(s9, j - 5)
        pl.when(j < chunks)(lambda: own_half(j))

        @pl.when(j == 1)
        def _():
            for u in range(2):
                for copy in col_copies(u):
                    copy.start()

        pl.when(late)(lambda: some_units(2 * (j - chunks) + 1))
        at_chunk(s2, j - 1)
        at_chunk(s4, j - 2)
        at_chunk(s6, j - 3)
        at_chunk(s8, j - 4)

    @pl.loop(0, chunks)
    def _(k):
        pl.when(k >= chunks - SLOTS)(lambda: reduced(k))
        for phase in (2, 3):
            for i in range(6):
                ring(phase, k, i).wait_send()
        for i in range(n):
            share(k, i).wait_send()

    @pl.loop(0, n)
    def _(o):
        swap(chunks - 1, o).wait_send()

    for u in (units - 2, units - 1):
        for copy in out_copies(u):
            copy.wait()


def solution(mesh):
    n = math.isqrt(mesh.shape["tp"] // 2)
    if n != 4 or 2 * n * n != mesh.shape["tp"]:
        raise ValueError("unexpected group")

    def step(x, dy, gate, up, w_gate, w_up, w_down):
        rows, width = x.shape
        ff = gate.shape[1]
        chunks, block = rows // (2 * HALF), width // n
        any_space = pl.BlockSpec(memory_space=pl.ANY)
        vmem = pl.BlockSpec(memory_space=pltpu.VMEM)
        dma = pltpu.SemaphoreType.DMA
        dx, dw_gate, dw_up, dw_down = pl.pallas_call(
            functools.partial(kernel, n),
            out_shape=(
                pltpu.VMEM(x.shape, BF16),
                jax.ShapeDtypeStruct(w_gate.shape, BF16),
                jax.ShapeDtypeStruct(w_up.shape, BF16),
                jax.ShapeDtypeStruct(w_down.shape, BF16),
            ),
            in_specs=[any_space] * 7,
            out_specs=(vmem, any_space, any_space, any_space),
            scratch_shapes=[
                pltpu.VMEM((ff, width), BF16),
                pltpu.VMEM((width, 2 * ff), BF16),
                pltpu.VMEM((rows, 2 * ff), BF16),
                pltpu.VMEM((ff, rows), BF16),
                pltpu.VMEM((SLOTS, n, HALF, block), BF16),
                pltpu.VMEM((n, HALF, block), BF16),
                pltpu.VMEM((2, HALF, width), BF16),
                pltpu.VMEM((2, HALF, ff), BF16),
                pltpu.VMEM((2, HALF, ff), BF16),
                pltpu.VMEM((2, rows, COLS), BF16),
                pltpu.VMEM((2, rows, COLS), BF16),
                pltpu.VMEM((2, COLS, 2 * ff), BF16),
                pltpu.VMEM((2, ff, COLS), BF16),
                dma((chunks, 4, 6)),
                dma((chunks, 4, 6)),
                dma((chunks, 2 * n)),
                dma((chunks, 2 * n)),
                pltpu.SemaphoreType.REGULAR((chunks,)),
                dma((3,)),
                dma((2, 3)),
                dma((2, 2)),
                dma((2, 3)),
            ],
            compiler_params=pltpu.CompilerParams(
                collective_id=0, has_side_effects=True, vmem_limit_bytes=700 * 64 * 1024
            ),
        )(x, dy, gate, up, w_gate, w_up, w_down)
        return dx, dw_gate, dw_up, dw_down

    tokens, columns, by_rows = P("dp", None), P(None, "tp"), P("tp", None)
    return jax.shard_map(
        step,
        mesh=mesh,
        in_specs=(tokens, tokens, P("dp", "tp"), P("dp", "tp"), columns, columns, by_rows),
        out_specs=(tokens, P("dp", "tp"), P("dp", "tp"), P(("dp", "tp"), None)),
        check_vma=False,
    )
```

time: 276 us -> 152 us (0.55)
  Pallas kernels: 0 us -> 134 us
  waiting for transfers between devices: 123 us -> 0 us
  matrix products: 108 us -> 0 us
  between operations: 14.1 us -> 0.65 us
  local copies, waits for them, and re-layouts: 30 us -> 17.3 us
    pallas_call x0 -> x1, Pallas kernels: none -> 134 us  [step(): pl.pallas_call(functools.partial(kernel, n), out_shape=(pltpu.VMEM(x.shap...]
    psum x1 -> x0, waiting for transfers between devices: 123 us -> none  [step(): dx = lax.psum(term.astype(jnp.bfloat16), 'tp')]
    dot_general x6 -> x0, matrix products: 108 us -> none  [the longest x1 24.1 us: step(): jnp.dot(d_up, w_up.T, preferred_element_type=jnp.float32)]
    unnamed x9 -> x10, local copies, waits for them, and re-layouts: 30 us -> 17.3 us
  transfers between devices with their start and end apart: 1 -> 0, of which waited for: 1 -> 0; matrix products, arithmetic and copies ran while one was open for 21% -> 0% of each run, Pallas kernels for 0% -> 0%
where the time goes in v1:
time: 152 us
  Pallas kernels  134 us (88%)
  local copies, waits for them, and re-layouts  17.3 us (11%)
    pallas_call x1, Pallas kernels, step(): pl.pallas_call(functools.partial(kernel, n), out_shape=(pltpu.VMEM(x.shap...  134 us
    unnamed x10, local copies, waits for them, and re-layouts  17.3 us

profile of v1, /device:TPU:97, one launch (start us, length us, event | category | flops | bytes accessed | tf_op | source)
XLA Modules:
  0.0 151.7 jit_solution(16235494622371088710)
XLA Ops:
  0.6 133.8 %shard_map.102 = (bf16[2048,5120]{1,0:T(8,128)(2,1)S(1)}, bf16[5120,384]{1,0:T(8,128)(2,1)}, bf16[5120,384]{1,0:T(8,128)(2,1)}, bf16[384,5120]{1,0:T(8,128)(2,1)}) custom-call(bf16[2048,5120]{1,0:T(8,128)(2,1)} %x.1, bf16[2048,5120]{1,0:T(8,128)(2,1)} %dy.1, bf16[2048,384]{1,0:T(8,128)(2,1)} %gate.1, bf16[2048,384]{1,0:T(8,128)(2,1)} %up.1, ...), custom_call_target="tpu_custom_call" | custom-call | tf_op jit(solution)/shard_map/pallas_call | solution.py:427
  134.4 0.0 copy-start.2
  134.4 8.3 %copy.15 = bf16[2048,5120]{1,0:T(8,128)(2,1)} copy(bf16[2048,5120]{1,0:T(8,128)(2,1)S(1)} %get-tuple-element.4) | data formatting | bytes 41943040
  142.7 0.0 copy-done.2
  142.7 0.0 copy-start.1
  142.7 2.0 %copy.16 = bf16[5120,384]{1,0:T(8,128)(2,1)} copy(bf16[5120,384]{1,0:T(8,128)(2,1)S(1)} %copy-done.2) | data formatting | bytes 7864320
  144.8 1.5 %copy-done.1 = bf16[5120,384]{1,0:T(8,128)(2,1)S(1)} copy-done((bf16[5120,384]{1,0:T(8,128)(2,1)S(1)}, bf16[5120,384]{1,0:T(8,128)(2,1)}, u32[]{:S(2)}) %copy-start.1) | copy-done | bytes 3932184
  146.3 0.0 copy-start
  146.3 2.0 %copy.17 = bf16[5120,384]{1,0:T(8,128)(2,1)} copy(bf16[5120,384]{1,0:T(8,128)(2,1)S(1)} %copy-done.1) | data formatting | bytes 7864320
  148.3 1.5 %copy-done = bf16[384,5120]{1,0:T(8,128)(2,1)S(1)} copy-done((bf16[384,5120]{1,0:T(8,128)(2,1)S(1)}, bf16[384,5120]{1,0:T(8,128)(2,1)}, u32[]{:S(2)}) %copy-start) | copy-done | bytes 3932184
  149.8 1.9 %copy.18 = bf16[384,5120]{1,0:T(8,128)(2,1)} copy(bf16[384,5120]{1,0:T(8,128)(2,1)S(1)} %copy-done) | data formatting | bytes 7864320
Async XLA Ops:
  134.4 8.3 %copy-start.2 = (bf16[5120,384]{1,0:T(8,128)(2,1)S(1)}, bf16[5120,384]{1,0:T(8,128)(2,1)}, u32[]{:S(2)}) copy-start(bf16[5120,384]{1,0:T(8,128)(2,1)} %get-tuple-element.13) | copy-start | bytes 11796484
  142.7 3.5 %copy-start.1 = (bf16[5120,384]{1,0:T(8,128)(2,1)S(1)}, bf16[5120,384]{1,0:T(8,128)(2,1)}, u32[]{:S(2)}) copy-start(bf16[5120,384]{1,0:T(8,128)(2,1)} %get-tuple-element.14) | copy-start | bytes 11796484
  146.3 3.5 %copy-start = (bf16[384,5120]{1,0:T(8,128)(2,1)S(1)}, bf16[384,5120]{1,0:T(8,128)(2,1)}, u32[]{:S(2)}) copy-start(bf16[384,5120]{1,0:T(8,128)(2,1)} %get-tuple-element.15) | copy-start | bytes 11796484

commit v2 on v1

v2 whole, which is shorter than its diff:
```python
import functools
import math

import jax
import jax.numpy as jnp
from jax import lax
from jax.experimental import pallas as pl
from jax.experimental.pallas import tpu as pltpu
from jax.sharding import PartitionSpec as P

MESH = pl.DeviceIdType.MESH
HALF = 256
SLOTS = 3
PERIOD = 10
TICKS = (
    (10, 20, 30, 40),
    (17, 27, 37, 45),
    (21, 31, 41, 48),
    (25, 35, 44, 51),
    (29, 39, 47, 54),
    (41, 43, 49, 57),
    (46, 50, 55, 61),
    (52, 57, 62, 66),
    (56, 62, 66, 70),
)
COLS = 256
F32, BF16 = jnp.float32, jnp.bfloat16
NT = (((1,), (1,)), ((), ()))
TN = (((0,), (0,)), ((), ()))
NN = (((1,), (0,)), ((), ()))


def dot(a, b, dims):
    return lax.dot_general(a, b, dims, preferred_element_type=F32)


def scoped(stage):
    def named(*args):
        with jax.named_scope(stage.__name__):
            return stage(*args)

    return named


def kernel(
    n, x, dy, gate, up, w_gate, w_up, w_down,
    wgu, wd, mine, theirs,
    dgu, hid, sums, outbox, dy_rows, g_rows, u_rows, x_cols, dy_cols,
    ring_send, ring_recv, pair_send, pair_recv, credit, w_sem, row_sem, col_sem,
):
    rows, width = x.shape
    ff = gate.shape[1]
    chunks = rows // (2 * HALF)
    block = width // n
    sub = HALF // n
    hr, hc = HALF // 2, block // 2
    units = width // COLS

    me = lax.axis_index("tp")
    c = lax.rem(me, 2)
    chip = me // 2
    px, py = chip // n, lax.rem(chip, n)
    p1 = px * (1 - c) + py * c
    p2 = py * (1 - c) + px * c

    def device(ax, ay, core):
        return (lax.rem(ax, n) * n + lax.rem(ay, n)) * 2 + core

    sx, sy = 1 - c, c
    right1, left1 = device(px + sx, py + sy, c), device(px + n - sx, py + n - sy, c)
    right2, left2 = device(px + sy, py + sx, c), device(px + n - sy, py + n - sx, c)
    partner = device(px, py, 1 - c)
    q1 = px * c + py * (1 - c)

    def mod(v):
        return lax.rem(v + n, n)

    def own(k):
        return pl.multiple_of((2 * k + c) * HALF, HALF)

    def other(k):
        return pl.multiple_of((2 * k + 1 - c) * HALF, HALF)

    def turn(o):
        return (2 + o) * (1 - o // 2) + (3 - o) * (o // 2)

    def kept(k):
        return pl.multiple_of(k * HALF, HALF)

    def cols(b):
        return pl.multiple_of(b * block, 128)

    def remote(src, dst, ssem, rsem, to):
        return pltpu.make_async_remote_copy(
            src_ref=src, dst_ref=dst, send_sem=ssem, recv_sem=rsem, device_id={"tp": to}, device_id_type=MESH
        )

    def rs1_src(k, b, h):
        return sums.at[lax.rem(k, SLOTS), b, pl.ds(h * hr, hr), :]

    def rs1_land(k, area, h):
        return theirs.at[pl.ds(kept(k) + h * hr, hr), pl.ds(area * block, block)]

    def rs2_src(k, s, h):
        return sums.at[lax.rem(k, SLOTS), p1, pl.ds(pl.multiple_of(s * sub, sub), sub), pl.ds(h * hc, hc)]

    def rs2_land(k, area, h):
        return theirs.at[pl.ds(kept(k) + area * sub, sub), pl.ds(3 * block + h * hc, hc)]

    def ag2_at(k, s, h):
        return mine.at[pl.ds(kept(k) + pl.multiple_of(s * sub, sub), sub), pl.ds(cols(p1) + h * hc, hc)]

    def ag1_at(k, b, h):
        return mine.at[pl.ds(kept(k) + h * hr, hr), pl.ds(cols(b), block)]

    land = {0: (0, 0), 1: (0, 1), 2: (1, 1), 3: (2, 0), 4: (1, 0), 5: (2, 1)}

    def reduce_pair(src, dst, p, i):
        which = {0: (2, 0), 1: (2, 1), 2: (n - 1, 1), 3: (1, 0), 4: (n - 1, 0), 5: (1, 1)}[i]
        return src(mod(p + which[0]), which[1]), dst(*land[i])

    def gather_at(at, p, i, arriving):
        off, h = {0: (0, 0), 1: (0, 1), 2: (0, 1), 3: (0, 0), 4: (1, 0), 5: (n - 1, 1)}[i]
        step = (1 if i % 2 == 0 else n - 1) if arriving else 0
        return at(mod(p + off + step), h)

    def ring(phase, k, i, arriving=False):
        left, right = (left1, right1) if phase in (0, 3) else (left2, right2)
        if phase == 0:
            src, dst = reduce_pair(functools.partial(rs1_src, k), functools.partial(rs1_land, k), p1, i)
        elif phase == 1:
            src, dst = reduce_pair(functools.partial(rs2_src, k), functools.partial(rs2_land, k), p2, i)
        elif phase == 2:
            src = dst = gather_at(functools.partial(ag2_at, k), p2, i, arriving)
        else:
            src = dst = gather_at(functools.partial(ag1_at, k), p1, i, arriving)
        to = left if i % 2 == 0 else right
        return remote(src, dst, ring_send.at[k, phase, i], ring_recv.at[k, phase, i], to)

    def send(phase, k, *which):
        for i in which:
            ring(phase, k, i).start()

    def arrive(phase, k, *which):
        for i in which:
            ring(phase, k, i, arriving=True).wait_recv()

    def reduced(k):
        for phase in (0, 1):
            for i in range(6):
                ring(phase, k, i).wait_send()

    def swap(k, o):
        b = lax.rem(q1 + turn(o), n)
        return remote(
            outbox.at[o], mine.at[pl.ds(kept(k), HALF), pl.ds(cols(b), block)],
            pair_send.at[k, o], pair_recv.at[k, o], partner,
        )

    def swap_in(k, o):
        b = lax.rem(p1 + turn(o), n)
        return remote(
            outbox.at[o], mine.at[pl.ds(kept(k), HALF), pl.ds(cols(b), block)],
            pair_send.at[k, o], pair_recv.at[k, o], partner,
        )

    def share(k, i):
        b = mod(p1 + (0, 1, n - 1, 2)[i])
        at = pl.ds(kept(k), HALF), pl.ds(cols(b), block)
        return remote(mine.at[at], theirs.at[at], pair_send.at[k, 4 + i], pair_recv.at[k, 4 + i], partner)

    def share_in(k, i):
        b = mod(q1 + (0, 1, n - 1, 2)[i])
        at = pl.ds(kept(k), HALF), pl.ds(cols(b), block)
        return remote(mine.at[at], theirs.at[at], pair_send.at[k, 4 + i], pair_recv.at[k, 4 + i], partner)

    def row_copies(b):
        at = pl.ds(pl.multiple_of((2 * (b // 2) + lax.rem(b + 1 + c, 2)) * HALF, HALF), HALF)
        slot = lax.rem(b, 2)
        return [
            pltpu.make_async_copy(src.at[at, :], dst.at[slot], row_sem.at[slot, i])
            for i, (src, dst) in enumerate(((dy, dy_rows), (gate, g_rows), (up, u_rows)))
        ]

    def col_copies(u):
        at = pl.ds(pl.multiple_of(u * COLS, COLS), COLS)
        slot = lax.rem(u, 2)
        return [
            pltpu.make_async_copy(src.at[:, at], dst.at[slot], col_sem.at[slot, i])
            for i, (src, dst) in enumerate(((x, x_cols), (dy, dy_cols)))
        ]

    load_wd = pltpu.make_async_copy(w_down, wd, w_sem.at[0])
    def load_w(i):
        at = pl.ds(pl.multiple_of(lax.rem(q1 + turn(i), n) * block, 128), block)
        return [
            pltpu.make_async_copy(w_gate.at[at, :], wgu.at[at, pl.ds(0, ff)], w_sem.at[2 * i + 1]),
            pltpu.make_async_copy(w_up.at[at, :], wgu.at[at, pl.ds(ff, ff)], w_sem.at[2 * i + 2]),
        ]

    @scoped
    def hidden_grads(b):
        for copy in row_copies(b):
            copy.wait()
        slot = lax.rem(b, 2)
        at = pl.multiple_of((2 * (b // 2) + lax.rem(b + 1 + c, 2)) * HALF, HALF)
        d_hidden = dot(dy_rows[slot], wd[...], NT)
        g, u = g_rows[slot].astype(F32), u_rows[slot].astype(F32)
        sig = jax.nn.sigmoid(g)
        silu = g * sig
        dgu[pl.ds(at, HALF), pl.ds(0, ff)] = (d_hidden * u * (sig + silu * (1.0 - sig))).astype(BF16)
        dgu[pl.ds(at, HALF), pl.ds(ff, ff)] = (d_hidden * silu).astype(BF16)
        hid[:, pl.ds(at, HALF)] = (silu * u).T.astype(BF16)

        @pl.when(b + 2 < 2 * chunks)
        def _():
            for copy in row_copies(b + 2):
                copy.start()

    def term(at, b):
        return dot(dgu[pl.ds(at, HALF), :], wgu[pl.ds(pl.multiple_of(b * block, 128), block), :], NT)

    @scoped
    def partner_block(k, o):
        @pl.when(jnp.logical_and(k == 0, o == 0))
        def _():
            for copy in load_w(0):
                copy.wait()

        @pl.when(jnp.logical_and(k == 0, o == 1))
        def _():
            for i in range(1, n):
                for copy in load_w(i):
                    copy.wait()

        pl.when(k > 0)(lambda: swap(k - 1, o).wait_send())
        outbox[o] = term(other(k), lax.rem(q1 + turn(o), n)).astype(BF16)
        swap(k, o).start()

    @scoped
    def own_block(k, o):
        pl.when(jnp.logical_and(k >= SLOTS, o == 0))(lambda: reduced(k - SLOTS))
        b = lax.rem(p1 + turn(o), n)
        t = term(own(k), b)
        swap_in(k, o).wait_recv()
        sums[lax.rem(k, SLOTS), b] = (t + mine[pl.ds(kept(k), HALF), pl.ds(cols(b), block)].astype(F32)).astype(BF16)
        pl.when(o == 0)(lambda: send(0, k, 0, 1))
        pl.when(o == 1)(lambda: send(0, k, 2))
        pl.when(o == 2)(lambda: send(0, k, 3))

    @scoped
    def weight_grads(u):
        for copy in col_copies(u):
            copy.wait()
        slot = lax.rem(u, 2)

        at = pl.ds(pl.multiple_of(u * COLS, COLS), COLS)
        wgu[at, :] = dot(x_cols[slot], dgu[...], TN).astype(BF16)
        wd[:, at] = dot(hid[...], dy_cols[slot], NN).astype(BF16)

        @pl.when(u + 2 < units)
        def _():
            for copy in col_copies(u + 2):
                copy.start()

    def add(dst, size, *srcs):
        step = 32

        @pl.loop(0, size // step)
        def _(r):
            at = pl.multiple_of(r * step, step)
            total = srcs[0](at, step).astype(F32)
            for s in srcs[1:]:
                total = total + s(at, step).astype(F32)
            dst(at, step, total.astype(BF16))

    def add_sums(k, b, off, size, lanes, *lands):
        def mine(at, step):
            return sums[lax.rem(k, SLOTS), b, pl.ds(off + at, step), lanes]

        def put(at, step, v):
            sums[lax.rem(k, SLOTS), b, pl.ds(off + at, step), lanes] = v

        add(put, size, mine, *lands)

    def landed(row, first, wide):
        return lambda at, step: theirs[pl.ds(row + at, step), pl.ds(first, wide)]

    @scoped
    def s1(k):
        arrive(0, k, 0)
        add_sums(k, mod(p1 + n - 1), 0, hr, slice(None), landed(kept(k), 0, block))
        send(0, k, 4)
        arrive(0, k, 1)
        add_sums(k, mod(p1 + 1), hr, hr, slice(None), landed(kept(k) + hr, 0, block))
        send(0, k, 5)

    @scoped
    def s2(k):
        arrive(0, k, 2, 3, 4, 5)
        add_sums(k, p1, 0, HALF, slice(None), landed(kept(k), block, block), landed(kept(k), 2 * block, block))
        send(1, k, 0, 1, 2, 3)

    @scoped
    def s3(k):
        base = 3 * block
        arrive(1, k, 0)
        add_sums(k, p1, pl.multiple_of(mod(p2 + n - 1) * sub, sub), sub, pl.ds(0, hc), landed(kept(k), base, hc))
        send(1, k, 4)
        arrive(1, k, 1)
        add_sums(k, p1, pl.multiple_of(mod(p2 + 1) * sub, sub), sub, pl.ds(hc, hc), landed(kept(k), base + hc, hc))
        send(1, k, 5)

    @scoped
    def s4(k):
        arrive(1, k, 2, 3, 4, 5)
        off = pl.multiple_of(p2 * sub, sub)

        def put(at, step, v):
            mine[pl.ds(kept(k) + off + at, step), pl.ds(cols(p1), block)] = v

        add(
            put, sub,
            lambda at, step: sums[lax.rem(k, SLOTS), p1, pl.ds(off + at, step), :],
            landed(kept(k) + sub, 3 * block, block),
            landed(kept(k) + 2 * sub, 3 * block, block),
        )
        send(2, k, 0, 1, 2, 3)
        pl.semaphore_signal(credit.at[k], inc=1, device_id={"tp": partner}, device_id_type=MESH)

    @scoped
    def s5(k):
        arrive(2, k, 0)
        send(2, k, 4)
        arrive(2, k, 1)
        send(2, k, 5)

    @scoped
    def s6(k):
        arrive(2, k, 2, 3, 4, 5)
        send(3, k, 0, 1, 2, 3)
        pl.semaphore_wait(credit.at[k], 1)
        share(k, 0).start()

    @scoped
    def s7(k):
        arrive(3, k, 0)
        send(3, k, 4)
        arrive(3, k, 1)
        send(3, k, 5)

    @scoped
    def s8(k):
        arrive(3, k, 2)
        share(k, 1).start()
        arrive(3, k, 3)
        share(k, 2).start()
        arrive(3, k, 4, 5)
        share(k, 3).start()

    @scoped
    def s9(k):
        for i in range(n):
            share_in(k, i).wait_recv()

    def matmuls(t):
        k, r = t // PERIOD, lax.rem(t, PERIOD)
        odd = lax.rem(r, 2) == 1
        last = r == PERIOD - 1

        pl.when(jnp.logical_or(r == 0, r == 2))(lambda: hidden_grads(2 * k + r // 2))
        pl.when(jnp.logical_and(odd, jnp.logical_not(last)))(lambda: partner_block(k, r // 2))
        pl.when(jnp.logical_or(last, jnp.logical_and(jnp.logical_not(odd), r >= 4)))(
            lambda: own_block(k, (r - 4 + r // (PERIOD - 1)) // 2)
        )

    stages = (s1, s2, s3, s4, s5, s6, s7, s8, s9)
    work = chunks * PERIOD

    load_wd.start()
    for copy in row_copies(0):
        copy.start()
    barrier = pltpu.get_barrier_semaphore()
    for to in (left1, right1, left2, right2, partner):
        pl.semaphore_signal(barrier, inc=1, device_id={"tp": to}, device_id_type=MESH)
    for copy in load_w(0) + row_copies(1) + load_w(1) + load_w(2) + load_w(3):
        copy.start()
    with jax.named_scope("meet"):
        pl.semaphore_wait(barrier, 5)
    with jax.named_scope("load"):
        load_wd.wait()

    @pl.loop(0, TICKS[-1][-1] + 1)
    def _(t):
        pl.when(t < work)(lambda: matmuls(t))

        @pl.when(t == PERIOD)
        def _():
            for u in range(2):
                for copy in col_copies(u):
                    copy.start()

        pl.when(jnp.logical_and(t >= work, t < work + units))(lambda: weight_grads(t - work))
        for stage, ticks in zip(stages, TICKS):
            now, k = t == ticks[0], 0
            for tick in ticks[1:]:
                now = jnp.logical_or(now, t == tick)
                k = k + (t >= tick).astype(jnp.int32)
            pl.when(now)(functools.partial(stage, k))

    @pl.loop(0, chunks)
    def _(k):
        pl.when(k >= chunks - SLOTS)(lambda: reduced(k))
        for phase in (2, 3):
            for i in range(6):
                ring(phase, k, i).wait_send()
        for i in range(n):
            share(k, i).wait_send()

    @pl.loop(0, n)
    def _(o):
        swap(chunks - 1, o).wait_send()


def store(dw_gu, dw_d, mine, theirs, dx, dw_gate, dw_up, dw_down, sem):
    c = lax.rem(lax.axis_index("tp"), 2)
    ff = dw_gate.shape[1]
    pairs = [(dw_gu.at[:, pl.ds(0, ff)], dw_gate), (dw_gu.at[:, pl.ds(ff, ff)], dw_up), (dw_d, dw_down)]
    for k in range(mine.shape[0] // HALF):
        for half, core in ((mine, c), (theirs, 1 - c)):
            at = pl.ds(pl.multiple_of((2 * k + core) * HALF, HALF), HALF)
            pairs.append((half.at[pl.ds(k * HALF, HALF), :], dx.at[at, :]))
    copies = [pltpu.make_async_copy(src, dst, sem.at[i]) for i, (src, dst) in enumerate(pairs)]
    for copy in copies:
        copy.start()
    for copy in copies:
        copy.wait()


def solution(mesh):
    n = math.isqrt(mesh.shape["tp"] // 2)
    if n != 4 or 2 * n * n != mesh.shape["tp"]:
        raise ValueError("unexpected group")

    def step(x, dy, gate, up, w_gate, w_up, w_down):
        rows, width = x.shape
        ff = gate.shape[1]
        chunks, block = rows // (2 * HALF), width // n
        any_space = pl.BlockSpec(memory_space=pl.ANY)
        vmem = pl.BlockSpec(memory_space=pltpu.VMEM)
        dma = pltpu.SemaphoreType.DMA
        kept = pl.pallas_call(
            functools.partial(kernel, n),
            out_shape=(
                pltpu.VMEM((width, 2 * ff), BF16),
                pltpu.VMEM((ff, width), BF16),
                pltpu.VMEM((rows // 2, width), BF16),
                pltpu.VMEM((rows // 2, width), BF16),
            ),
            in_specs=[any_space] * 7,
            out_specs=[vmem] * 4,
            scratch_shapes=[
                pltpu.VMEM((rows, 2 * ff), BF16),
                pltpu.VMEM((ff, rows), BF16),
                pltpu.VMEM((SLOTS, n, HALF, block), BF16),
                pltpu.VMEM((n, HALF, block), BF16),
                pltpu.VMEM((2, HALF, width), BF16),
                pltpu.VMEM((2, HALF, ff), BF16),
                pltpu.VMEM((2, HALF, ff), BF16),
                pltpu.VMEM((2, rows, COLS), BF16),
                pltpu.VMEM((2, rows, COLS), BF16),
                dma((chunks, 4, 6)),
                dma((chunks, 4, 6)),
                dma((chunks, 2 * n)),
                dma((chunks, 2 * n)),
                pltpu.SemaphoreType.REGULAR((chunks,)),
                dma((1 + 2 * n,)),
                dma((2, 3)),
                dma((2, 2)),
            ],
            compiler_params=pltpu.CompilerParams(
                collective_id=0, has_side_effects=True, vmem_limit_bytes=31 * 1024 * 1024
            ),
        )(x, dy, gate, up, w_gate, w_up, w_down)
        return pl.pallas_call(
            store,
            out_shape=[jax.ShapeDtypeStruct(a.shape, BF16) for a in (x, w_gate, w_up, w_down)],
            in_specs=[vmem] * 4,
            out_specs=[any_space] * 4,
            scratch_shapes=[dma((3 + rows // HALF,))],
            compiler_params=pltpu.CompilerParams(vmem_limit_bytes=1024 * 1024),
        )(*kept)

    tokens, columns, by_rows = P("dp", None), P(None, "tp"), P("tp", None)
    return jax.shard_map(
        step,
        mesh=mesh,
        in_specs=(tokens, tokens, P("dp", "tp"), P("dp", "tp"), columns, columns, by_rows),
        out_specs=(tokens, P("dp", "tp"), P("dp", "tp"), P(("dp", "tp"), None)),
        check_vma=False,
    )
```

time: 152 us -> 140 us (0.921)
  local copies, waits for them, and re-layouts: 17.3 us -> 0 us
  Pallas kernels: 134 us -> 139 us
    unnamed x10 -> x0, local copies, waits for them, and re-layouts: 17.3 us -> none
    pallas_call x1 -> x2, Pallas kernels: 134 us -> 139 us  [the longest x1 128 us: step(): pl.pallas_call(functools.partial(kernel, n), out_shape=(pltpu.VMEM((width...]
where the time goes in v2:
time: 140 us
  Pallas kernels  139 us (99%)
    pallas_call x1, Pallas kernels, step(): pl.pallas_call(functools.partial(kernel, n), out_shape=(pltpu.VMEM((width...  128 us
    pallas_call x1, Pallas kernels, step(): pl.pallas_call(store, out_shape=[jax.ShapeDtypeStruct(a.shape, BF16) for...  10.9 us

profile of v2, /device:TPU:97, one launch (start us, length us, event | category | flops | bytes accessed | tf_op | source)
XLA Modules:
  0.0 139.5 jit_solution(17960849660565446319)
XLA Ops:
  0.6 128.0 %shard_map.102 = (bf16[5120,768]{1,0:T(8,128)(2,1)S(1)}, bf16[384,5120]{1,0:T(8,128)(2,1)S(1)}, bf16[1024,5120]{1,0:T(8,128)(2,1)S(1)}, bf16[1024,5120]{1,0:T(8,128)(2,1)S(1)}) custom-call(bf16[2048,5120]{1,0:T(8,128)(2,1)} %x.1, bf16[2048,5120]{1,0:T(8,128)(2,1)} %dy.1, bf16[2048,384]{1,0:T(8,128)(2,1)} %gate.1, bf16[2048,384]{1,0:T(8,128)(2,1)} %up.1, ...), custom_call_target="tpu_custom_call" | custom-call | tf_op jit(solution)/shard_map/pallas_call | solution.py:452
  128.6 10.9 %shard_map.103 = (bf16[2048,5120]{1,0:T(8,128)(2,1)}, bf16[5120,384]{1,0:T(8,128)(2,1)}, bf16[5120,384]{1,0:T(8,128)(2,1)}, bf16[384,5120]{1,0:T(8,128)(2,1)}) custom-call(bf16[5120,768]{1,0:T(8,128)(2,1)S(1)} %get-tuple-element.8.dw_gu, bf16[384,5120]{1,0:T(8,128)(2,1)S(1)} %get-tuple-element.9.dw_d, bf16[1024,5120]{1,0:T(8,128)(2,1)S(1)} %get-tuple-element.10.mine, ...), custom_call_target="tpu_custom_call" | custom-call | tf_op jit(solution)/shard_map/pallas_call | solution.py:485

commit v3 on v2

--- a/solution.py
+++ b/solution.py
@@ -18,11 +18,12 @@
     (21, 31, 41, 48),
     (25, 35, 44, 51),
     (29, 39, 47, 54),
-    (41, 43, 49, 57),
-    (46, 50, 55, 61),
-    (52, 57, 62, 66),
-    (56, 62, 66, 70),
+    (41, 45, 52, 57),
+    (48, 54, 60, 64),
+    (54, 60, 65, 70),
+    (58, 64, 70, 75),
 )
+PIECES = 4
 COLS = 256
 F32, BF16 = jnp.float32, jnp.bfloat16
 NT = (((1,), (1,)), ((), ()))
@@ -46,7 +47,7 @@
     n, x, dy, gate, up, w_gate, w_up, w_down,
     wgu, wd, mine, theirs,
     dgu, hid, sums, outbox, dy_rows, g_rows, u_rows, x_cols, dy_cols,
-    ring_send, ring_recv, pair_send, pair_recv, credit, w_sem, row_sem, col_sem,
+    ring_send, ring_recv, pair_send, pair_recv, credit, w_sem, first_sem, row_sem, col_sem,
 ):
     rows, width = x.shape
     ff = gate.shape[1]
@@ -164,22 +165,29 @@
             pair_send.at[k, o], pair_recv.at[k, o], partner,
         )
 
+    def shared(k, i, place):
+        b = mod(place + (0, 1, n - 1, 2, 2)[i])
+        first, size = ((0, HALF), (0, HALF), (0, HALF), (0, hr), (hr, hr))[i]
+        return pl.ds(kept(k) + first, size), pl.ds(cols(b), block)
+
     def share(k, i):
-        b = mod(p1 + (0, 1, n - 1, 2)[i])
-        at = pl.ds(kept(k), HALF), pl.ds(cols(b), block)
+        at = shared(k, i, p1)
         return remote(mine.at[at], theirs.at[at], pair_send.at[k, 4 + i], pair_recv.at[k, 4 + i], partner)
 
     def share_in(k, i):
-        b = mod(q1 + (0, 1, n - 1, 2)[i])
-        at = pl.ds(kept(k), HALF), pl.ds(cols(b), block)
+        at = shared(k, i, q1)
         return remote(mine.at[at], theirs.at[at], pair_send.at[k, 4 + i], pair_recv.at[k, 4 + i], partner)
 
-    def row_copies(b):
-        at = pl.ds(pl.multiple_of((2 * (b // 2) + lax.rem(b + 1 + c, 2)) * HALF, HALF), HALF)
+    def rows_of(b):
+        return pl.multiple_of((2 * (b // 2) + lax.rem(b + 1 + c, 2)) * HALF, HALF)
+
+    def row_copies(b, first=0):
+        at = pl.ds(rows_of(b), HALF)
         slot = lax.rem(b, 2)
         return [
             pltpu.make_async_copy(src.at[at, :], dst.at[slot], row_sem.at[slot, i])
             for i, (src, dst) in enumerate(((dy, dy_rows), (gate, g_rows), (up, u_rows)))
+            if i >= first
         ]
 
     def col_copies(u):
@@ -194,17 +202,12 @@
     def load_w(i):
         at = pl.ds(pl.multiple_of(lax.rem(q1 + turn(i), n) * block, 128), block)
         return [
-            pltpu.make_async_copy(w_gate.at[at, :], wgu.at[at, pl.ds(0, ff)], w_sem.at[2 * i + 1]),
-            pltpu.make_async_copy(w_up.at[at, :], wgu.at[at, pl.ds(ff, ff)], w_sem.at[2 * i + 2]),
+            pltpu.make_async_copy(w_gate.at[at, :], wgu.at[at, pl.ds(0, ff)], w_sem.at[i, 0]),
+            pltpu.make_async_copy(w_up.at[at, :], wgu.at[at, pl.ds(ff, ff)], w_sem.at[i, 1]),
         ]
 
-    @scoped
-    def hidden_grads(b):
-        for copy in row_copies(b):
-            copy.wait()
-        slot = lax.rem(b, 2)
-        at = pl.multiple_of((2 * (b // 2) + lax.rem(b + 1 + c, 2)) * HALF, HALF)
-        d_hidden = dot(dy_rows[slot], wd[...], NT)
+    def split_grads(b, d_hidden):
+        slot, at = lax.rem(b, 2), rows_of(b)
         g, u = g_rows[slot].astype(F32), u_rows[slot].astype(F32)
         sig = jax.nn.sigmoid(g)
         silu = g * sig
@@ -212,10 +215,41 @@
         dgu[pl.ds(at, HALF), pl.ds(ff, ff)] = (d_hidden * silu).astype(BF16)
         hid[:, pl.ds(at, HALF)] = (silu * u).T.astype(BF16)
 
+    @scoped
+    def hidden_grads(b):
+        for copy in row_copies(b):
+            copy.wait()
+        split_grads(b, dot(dy_rows[lax.rem(b, 2)], wd[...], NT))
+
         @pl.when(b + 2 < 2 * chunks)
         def _():
             for copy in row_copies(b + 2):
                 copy.start()
+
+    def first_copies(i):
+        at = pl.ds(i * (width // PIECES), width // PIECES)
+        return [
+            pltpu.make_async_copy(dy.at[pl.ds(rows_of(0), HALF), at], dy_rows.at[0, :, at], first_sem.at[i, 0]),
+            pltpu.make_async_copy(w_down.at[:, at], wd.at[:, at], first_sem.at[i, 1]),
+        ]
+
+    @scoped
+    def first_grads():
+        behind = [load_w(0), row_copies(1), load_w(1), load_w(2) + load_w(3)]
+        d_hidden = None
+        for i in range(PIECES):
+            for copy in first_copies(i):
+                copy.wait()
+            for copy in behind[i]:
+                copy.start()
+            at = pl.ds(i * (width // PIECES), width // PIECES)
+            part = dot(dy_rows[0, :, at], wd[:, at], NT)
+            d_hidden = part if d_hidden is None else d_hidden + part
+        for copy in row_copies(0, first=1):
+            copy.wait()
+        split_grads(0, d_hidden)
+        for copy in row_copies(2):
+            copy.start()
 
     def term(at, b):
         return dot(dgu[pl.ds(at, HALF), :], wgu[pl.ds(pl.multiple_of(b * block, 128), block), :], NT)
@@ -355,40 +389,41 @@
         share(k, 1).start()
         arrive(3, k, 3)
         share(k, 2).start()
-        arrive(3, k, 4, 5)
+        arrive(3, k, 4)
         share(k, 3).start()
+        arrive(3, k, 5)
+        share(k, 4).start()
 
     @scoped
     def s9(k):
-        for i in range(n):
+        for i in range(5):
             share_in(k, i).wait_recv()
 
     def matmuls(t):
         k, r = t // PERIOD, lax.rem(t, PERIOD)
-        odd = lax.rem(r, 2) == 1
-        last = r == PERIOD - 1
-
-        pl.when(jnp.logical_or(r == 0, r == 2))(lambda: hidden_grads(2 * k + r // 2))
-        pl.when(jnp.logical_and(odd, jnp.logical_not(last)))(lambda: partner_block(k, r // 2))
-        pl.when(jnp.logical_or(last, jnp.logical_and(jnp.logical_not(odd), r >= 4)))(
-            lambda: own_block(k, (r - 4 + r // (PERIOD - 1)) // 2)
-        )
+        first = r < 4
+        even = lax.rem(r, 2) == 0
+        to_partner = jnp.logical_or(r == 1, jnp.logical_or(r == 3, jnp.logical_or(r == 5, r == 7)))
+        to_own = jnp.logical_or(r == 4, jnp.logical_or(r == 6, r >= 8))
+        grads = jnp.logical_and(first, even)
+        pl.when(jnp.logical_and(grads, t > 0))(lambda: hidden_grads(2 * k + r // 2))
+        pl.when(to_partner)(lambda: partner_block(k, r // 2))
+        pl.when(to_own)(lambda: own_block(k, r // 6 + r // 8 + r // 9))
 
     stages = (s1, s2, s3, s4, s5, s6, s7, s8, s9)
     work = chunks * PERIOD
 
-    load_wd.start()
-    for copy in row_copies(0):
-        copy.start()
     barrier = pltpu.get_barrier_semaphore()
     for to in (left1, right1, left2, right2, partner):
         pl.semaphore_signal(barrier, inc=1, device_id={"tp": to}, device_id_type=MESH)
-    for copy in load_w(0) + row_copies(1) + load_w(1) + load_w(2) + load_w(3):
+    for i in range(PIECES):
+        for copy in first_copies(i):
+            copy.start()
+    for copy in row_copies(0, first=1):
         copy.start()
+    first_grads()
     with jax.named_scope("meet"):
         pl.semaphore_wait(barrier, 5)
-    with jax.named_scope("load"):
-        load_wd.wait()
 
     @pl.loop(0, TICKS[-1][-1] + 1)
     def _(t):
@@ -414,7 +449,7 @@
         for phase in (2, 3):
             for i in range(6):
                 ring(phase, k, i).wait_send()
-        for i in range(n):
+        for i in range(5):
             share(k, i).wait_send()
 
     @pl.loop(0, n)
@@ -471,10 +506,11 @@
                 pltpu.VMEM((2, rows, COLS), BF16),
                 dma((chunks, 4, 6)),
                 dma((chunks, 4, 6)),
-                dma((chunks, 2 * n)),
-                dma((chunks, 2 * n)),
+                dma((chunks, n + 5)),
+                dma((chunks, n + 5)),
                 pltpu.SemaphoreType.REGULAR((chunks,)),
-                dma((1 + 2 * n,)),
+                dma((n, 2)),
+                dma((PIECES, 2)),
                 dma((2, 3)),
                 dma((2, 2)),
             ],

time: 140 us -> 139 us (level)
  no operation moved by 1% of the time
where the time goes in v3:
time: 139 us
  Pallas kernels  138 us (99%)
    pallas_call x1, Pallas kernels, step(): pl.pallas_call(functools.partial(kernel, n), out_shape=(pltpu.VMEM((width...  127 us
    pallas_call x1, Pallas kernels, step(): pl.pallas_call(store, out_shape=[jax.ShapeDtypeStruct(a.shape, BF16) for...  10.9 us

profile of v3, /device:TPU:97, one launch (start us, length us, event | category | flops | bytes accessed | tf_op | source)
XLA Modules:
  0.0 138.6 jit_solution(5759977959674938972)
XLA Ops:
  0.6 127.0 %shard_map.102 = (bf16[5120,768]{1,0:T(8,128)(2,1)S(1)}, bf16[384,5120]{1,0:T(8,128)(2,1)S(1)}, bf16[1024,5120]{1,0:T(8,128)(2,1)S(1)}, bf16[1024,5120]{1,0:T(8,128)(2,1)S(1)}) custom-call(bf16[2048,5120]{1,0:T(8,128)(2,1)} %x.1, bf16[2048,5120]{1,0:T(8,128)(2,1)} %dy.1, bf16[2048,384]{1,0:T(8,128)(2,1)} %gate.1, bf16[2048,384]{1,0:T(8,128)(2,1)} %up.1, ...), custom_call_target="tpu_custom_call" | custom-call | tf_op jit(solution)/shard_map/pallas_call | solution.py:487
  127.7 10.9 %shard_map.103 = (bf16[2048,5120]{1,0:T(8,128)(2,1)}, bf16[5120,384]{1,0:T(8,128)(2,1)}, bf16[5120,384]{1,0:T(8,128)(2,1)}, bf16[384,5120]{1,0:T(8,128)(2,1)}) custom-call(bf16[5120,768]{1,0:T(8,128)(2,1)S(1)} %get-tuple-element.8.dw_gu, bf16[384,5120]{1,0:T(8,128)(2,1)S(1)} %get-tuple-element.9.dw_d, bf16[1024,5120]{1,0:T(8,128)(2,1)S(1)} %get-tuple-element.10.mine, ...), custom_call_target="tpu_custom_call" | custom-call | tf_op jit(solution)/shard_map/pallas_call | solution.py:521

commit v4 on v3

--- a/solution.py
+++ b/solution.py
@@ -47,7 +47,7 @@
     n, x, dy, gate, up, w_gate, w_up, w_down,
     wgu, wd, mine, theirs,
     dgu, hid, sums, outbox, dy_rows, g_rows, u_rows, x_cols, dy_cols,
-    ring_send, ring_recv, pair_send, pair_recv, credit, w_sem, first_sem, row_sem, col_sem,
+    ring_send, ring_recv, swap_send, share_send, pair_recv, credit, w_sem, first_sem, row_sem, col_sem,
 ):
     rows, width = x.shape
     ff = gate.shape[1]
@@ -111,8 +111,27 @@
     def ag2_at(k, s, h):
         return mine.at[pl.ds(kept(k) + pl.multiple_of(s * sub, sub), sub), pl.ds(cols(p1) + h * hc, hc)]
 
-    def ag1_at(k, b, h):
-        return mine.at[pl.ds(kept(k) + h * hr, hr), pl.ds(cols(b), block)]
+    late = (0, 1, n - 1, 2)
+
+    def ag1_at(k, b, o):
+        at = pl.multiple_of(mod(p2 + late[o]) * sub, sub)
+        return mine.at[pl.ds(kept(k) + at, sub), pl.ds(cols(b), block)]
+
+    arrivals = (
+        (0, 1, 2, 2, 2, 2),
+        (3, 4, 5, 5, 5, 5),
+        (6, 7, 8, 9, 10, 10),
+        (11, 16, 13, 16, 15, 12, 15, 14, 17, 18, 19, 20),
+    )
+
+    def together(ref, ssem, rsem):
+        return remote(ref, ref, ssem, rsem, partner)
+
+    def arrive_together(phase, k, i, ref):
+        together(ref, ring_send.at[k, phase], ring_recv.at[k, arrivals[phase][i]]).wait_recv()
+
+    def left_together(phase, k, ref):
+        together(ref, ring_send.at[k, phase], ring_recv.at[k, 0]).wait_send()
 
     land = {0: (0, 0), 1: (0, 1), 2: (1, 1), 3: (2, 0), 4: (1, 0), 5: (2, 1)}
 
@@ -134,9 +153,10 @@
         elif phase == 2:
             src = dst = gather_at(functools.partial(ag2_at, k), p2, i, arriving)
         else:
-            src = dst = gather_at(functools.partial(ag1_at, k), p1, i, arriving)
+            o, off = (i // 2, 0) if i < 8 else (i // 2 - 4 + 2 * (i % 2), (1, n - 1)[i % 2])
+            src = dst = ag1_at(k, mod(p1 + off + ((1, n - 1)[i % 2] if arriving else 0)), o)
         to = left if i % 2 == 0 else right
-        return remote(src, dst, ring_send.at[k, phase, i], ring_recv.at[k, phase, i], to)
+        return remote(src, dst, ring_send.at[k, phase], ring_recv.at[k, arrivals[phase][i]], to)
 
     def send(phase, k, *which):
         for i in which:
@@ -147,36 +167,33 @@
             ring(phase, k, i, arriving=True).wait_recv()
 
     def reduced(k):
-        for phase in (0, 1):
-            for i in range(6):
-                ring(phase, k, i).wait_send()
+        left_together(0, k, sums.at[lax.rem(k, SLOTS), pl.ds(0, 3)])
+        left_together(1, k, sums.at[lax.rem(k, SLOTS), 0, pl.ds(0, 3 * sub), :])
 
     def swap(k, o):
         b = lax.rem(q1 + turn(o), n)
         return remote(
             outbox.at[o], mine.at[pl.ds(kept(k), HALF), pl.ds(cols(b), block)],
-            pair_send.at[k, o], pair_recv.at[k, o], partner,
+            swap_send.at[o], pair_recv.at[k, o], partner,
         )
 
     def swap_in(k, o):
         b = lax.rem(p1 + turn(o), n)
         return remote(
             outbox.at[o], mine.at[pl.ds(kept(k), HALF), pl.ds(cols(b), block)],
-            pair_send.at[k, o], pair_recv.at[k, o], partner,
+            swap_send.at[o], pair_recv.at[k, o], partner,
         )
 
-    def shared(k, i, place):
-        b = mod(place + (0, 1, n - 1, 2, 2)[i])
-        first, size = ((0, HALF), (0, HALF), (0, HALF), (0, hr), (hr, hr))[i]
-        return pl.ds(kept(k) + first, size), pl.ds(cols(b), block)
+    def shared(k, i, place, piece):
+        b = mod(place + (0, 1, n - 1, 2, 2, 2, 2)[i])
+        if i < 3:
+            return pl.ds(kept(k), HALF), pl.ds(cols(b), block)
+        at = pl.multiple_of(mod(piece + late[i - 3]) * sub, sub)
+        return pl.ds(kept(k) + at, sub), pl.ds(cols(b), block)
 
     def share(k, i):
-        at = shared(k, i, p1)
-        return remote(mine.at[at], theirs.at[at], pair_send.at[k, 4 + i], pair_recv.at[k, 4 + i], partner)
-
-    def share_in(k, i):
-        at = shared(k, i, q1)
-        return remote(mine.at[at], theirs.at[at], pair_send.at[k, 4 + i], pair_recv.at[k, 4 + i], partner)
+        at = shared(k, i, p1, p2)
+        return remote(mine.at[at], theirs.at[at], share_send.at[k], pair_recv.at[k, n], partner)
 
     def rows_of(b):
         return pl.multiple_of((2 * (b // 2) + lax.rem(b + 1 + c, 2)) * HALF, HALF)
@@ -184,10 +201,9 @@
     def row_copies(b, first=0):
         at = pl.ds(rows_of(b), HALF)
         slot = lax.rem(b, 2)
+        pairs = ((dy, dy_rows), (gate, g_rows), (up, u_rows))
         return [
-            pltpu.make_async_copy(src.at[at, :], dst.at[slot], row_sem.at[slot, i])
-            for i, (src, dst) in enumerate(((dy, dy_rows), (gate, g_rows), (up, u_rows)))
-            if i >= first
+            pltpu.make_async_copy(pairs[i][0].at[at, :], pairs[i][1].at[slot], row_sem.at[slot, i]) for i in range(first, 3)
         ]
 
     def col_copies(u):
@@ -322,6 +338,11 @@
 
     @scoped
     def s1(k):
+        @pl.when(k == chunks - 1)
+        def _():
+            for o in range(n):
+                swap(k, o).wait_send()
+
         arrive(0, k, 0)
         add_sums(k, mod(p1 + n - 1), 0, hr, slice(None), landed(kept(k), 0, block))
         send(0, k, 4)
@@ -331,7 +352,7 @@
 
     @scoped
     def s2(k):
-        arrive(0, k, 2, 3, 4, 5)
+        arrive_together(0, k, 2, theirs.at[pl.ds(kept(k), HALF), pl.ds(block, 2 * block)])
         add_sums(k, p1, 0, HALF, slice(None), landed(kept(k), block, block), landed(kept(k), 2 * block, block))
         send(1, k, 0, 1, 2, 3)
 
@@ -347,7 +368,7 @@
 
     @scoped
     def s4(k):
-        arrive(1, k, 2, 3, 4, 5)
+        arrive_together(1, k, 2, theirs.at[pl.ds(kept(k) + sub, 2 * sub), pl.ds(3 * block, block)])
         off = pl.multiple_of(p2 * sub, sub)
 
         def put(at, step, v):
@@ -360,6 +381,7 @@
             landed(kept(k) + 2 * sub, 3 * block, block),
         )
         send(2, k, 0, 1, 2, 3)
+        pl.when(k == chunks - 1)(lambda: send(3, k, 0, 1))
         pl.semaphore_signal(credit.at[k], inc=1, device_id={"tp": partner}, device_id_type=MESH)
 
     @scoped
@@ -371,33 +393,40 @@
 
     @scoped
     def s6(k):
-        arrive(2, k, 2, 3, 4, 5)
-        send(3, k, 0, 1, 2, 3)
+        pl.when(k < chunks - 1)(lambda: send(3, k, 0, 1))
+        arrive(2, k, 2)
+        send(3, k, 2)
+        arrive(2, k, 3)
+        send(3, k, 4, 5)
+        arrive_together(2, k, 4, mine.at[pl.ds(kept(k), sub), pl.ds(cols(p1), block)])
+        send(3, k, 6, 7, 3)
         pl.semaphore_wait(credit.at[k], 1)
         share(k, 0).start()
 
     @scoped
     def s7(k):
-        arrive(3, k, 0)
-        send(3, k, 4)
-        arrive(3, k, 1)
-        send(3, k, 5)
+        for came, on in ((0, 8), (5, 9), (2, 10), (7, 11)):
+            arrive(3, k, came)
+            send(3, k, on)
 
     @scoped
     def s8(k):
-        arrive(3, k, 2)
+        pl.when(k >= chunks - SLOTS)(lambda: reduced(k))
+        left_together(2, k, mine.at[pl.ds(kept(k), 3 * sub), pl.ds(0, block)])
+        arrive_together(3, k, 4, mine.at[pl.ds(kept(k), hr), pl.ds(cols(mod(p1 + 1)), block)])
         share(k, 1).start()
-        arrive(3, k, 3)
+        arrive_together(3, k, 1, mine.at[pl.ds(kept(k), hr), pl.ds(cols(mod(p1 + n - 1)), block)])
         share(k, 2).start()
-        arrive(3, k, 4)
-        share(k, 3).start()
-        arrive(3, k, 5)
-        share(k, 4).start()
+        for came, i in ((8, 3), (9, 5), (10, 4), (11, 6)):
+            arrive(3, k, came)
+            share(k, i).start()
 
     @scoped
     def s9(k):
-        for i in range(5):
-            share_in(k, i).wait_recv()
+        whole = pl.ds(kept(k), HALF)
+        together(theirs.at[whole, :], share_send.at[k], pair_recv.at[k, n]).wait_recv()
+        left_together(3, k, sums.at[lax.rem(k, SLOTS), pl.ds(0, 3)])
+        together(mine.at[whole, :], share_send.at[k], pair_recv.at[k, n]).wait_send()
 
     def matmuls(t):
         k, r = t // PERIOD, lax.rem(t, PERIOD)
@@ -442,19 +471,6 @@
                 now = jnp.logical_or(now, t == tick)
                 k = k + (t >= tick).astype(jnp.int32)
             pl.when(now)(functools.partial(stage, k))
-
-    @pl.loop(0, chunks)
-    def _(k):
-        pl.when(k >= chunks - SLOTS)(lambda: reduced(k))
-        for phase in (2, 3):
-            for i in range(6):
-                ring(phase, k, i).wait_send()
-        for i in range(5):
-            share(k, i).wait_send()
-
-    @pl.loop(0, n)
-    def _(o):
-        swap(chunks - 1, o).wait_send()
 
 
 def store(dw_gu, dw_d, mine, theirs, dx, dw_gate, dw_up, dw_down, sem):
@@ -504,10 +520,11 @@
                 pltpu.VMEM((2, HALF, ff), BF16),
                 pltpu.VMEM((2, rows, COLS), BF16),
                 pltpu.VMEM((2, rows, COLS), BF16),
-                dma((chunks, 4, 6)),
-                dma((chunks, 4, 6)),
-                dma((chunks, n + 5)),
-                dma((chunks, n + 5)),
+                dma((chunks, 4)),
+                dma((chunks, 21)),
+                dma((n,)),
+                dma((chunks,)),
+                dma((chunks, n + 1)),
                 pltpu.SemaphoreType.REGULAR((chunks,)),
                 dma((n, 2)),
                 dma((PIECES, 2)),

time: 139 us -> 137 us (0.986)
  Pallas kernels: 138 us -> 136 us
    pallas_call x1, Pallas kernels: 127 us -> 126 us  [step(): pl.pallas_call(functools.partial(kernel, n), out_shape=(pltpu.VMEM((width...]
where the time goes in v4:
time: 137 us
  Pallas kernels  136 us (99%)
    pallas_call x1, Pallas kernels, step(): pl.pallas_call(functools.partial(kernel, n), out_shape=(pltpu.VMEM((width...  126 us
    pallas_call x1, Pallas kernels, step(): pl.pallas_call(store, out_shape=[jax.ShapeDtypeStruct(a.shape, BF16) for...  10.9 us

profile of v4, /device:TPU:97, one launch (start us, length us, event | category | flops | bytes accessed | tf_op | source)
XLA Modules:
  0.0 137.1 jit_solution(11933683907960015476)
XLA Ops:
  0.6 125.5 %shard_map.102 = (bf16[5120,768]{1,0:T(8,128)(2,1)S(1)}, bf16[384,5120]{1,0:T(8,128)(2,1)S(1)}, bf16[1024,5120]{1,0:T(8,128)(2,1)S(1)}, bf16[1024,5120]{1,0:T(8,128)(2,1)S(1)}) custom-call(bf16[2048,5120]{1,0:T(8,128)(2,1)} %x.1, bf16[2048,5120]{1,0:T(8,128)(2,1)} %dy.1, bf16[2048,384]{1,0:T(8,128)(2,1)} %gate.1, bf16[2048,384]{1,0:T(8,128)(2,1)} %up.1, ...), custom_call_target="tpu_custom_call" | custom-call | tf_op jit(solution)/shard_map/pallas_call | solution.py:503
  126.2 10.9 %shard_map.103 = (bf16[2048,5120]{1,0:T(8,128)(2,1)}, bf16[5120,384]{1,0:T(8,128)(2,1)}, bf16[5120,384]{1,0:T(8,128)(2,1)}, bf16[384,5120]{1,0:T(8,128)(2,1)}) custom-call(bf16[5120,768]{1,0:T(8,128)(2,1)S(1)} %get-tuple-element.8.dw_gu, bf16[384,5120]{1,0:T(8,128)(2,1)S(1)} %get-tuple-element.9.dw_d, bf16[1024,5120]{1,0:T(8,128)(2,1)S(1)} %get-tuple-element.10.mine, ...), custom_call_target="tpu_custom_call" | custom-call | tf_op jit(solution)/shard_map/pallas_call | solution.py:538

commit v5 on v4

--- a/solution.py
+++ b/solution.py
@@ -218,8 +218,8 @@
     def load_w(i):
         at = pl.ds(pl.multiple_of(lax.rem(q1 + turn(i), n) * block, 128), block)
         return [
-            pltpu.make_async_copy(w_gate.at[at, :], wgu.at[at, pl.ds(0, ff)], w_sem.at[i, 0]),
-            pltpu.make_async_copy(w_up.at[at, :], wgu.at[at, pl.ds(ff, ff)], w_sem.at[i, 1]),
+            pltpu.make_async_copy(w_gate.at[at, :], wgu.at[at, pl.ds(0, ff)], w_sem.at[min(i, 1)]),
+            pltpu.make_async_copy(w_up.at[at, :], wgu.at[at, pl.ds(ff, ff)], w_sem.at[min(i, 1)]),
         ]
 
     def split_grads(b, d_hidden):
@@ -230,6 +230,10 @@
         dgu[pl.ds(at, HALF), pl.ds(0, ff)] = (d_hidden * u * (sig + silu * (1.0 - sig))).astype(BF16)
         dgu[pl.ds(at, HALF), pl.ds(ff, ff)] = (d_hidden * silu).astype(BF16)
         hid[:, pl.ds(at, HALF)] = (silu * u).T.astype(BF16)
+
+    def loaded(sem, blocks):
+        at = pl.ds(0, blocks * block)
+        pltpu.make_async_copy(wgu.at[at, :], wgu.at[at, :], w_sem.at[sem]).wait()
 
     @scoped
     def hidden_grads(b):
@@ -274,14 +278,11 @@
     def partner_block(k, o):
         @pl.when(jnp.logical_and(k == 0, o == 0))
         def _():
-            for copy in load_w(0):
-                copy.wait()
+            loaded(0, 1)
 
         @pl.when(jnp.logical_and(k == 0, o == 1))
         def _():
-            for i in range(1, n):
-                for copy in load_w(i):
-                    copy.wait()
+            loaded(1, n - 1)
 
         pl.when(k > 0)(lambda: swap(k - 1, o).wait_send())
         outbox[o] = term(other(k), lax.rem(q1 + turn(o), n)).astype(BF16)
@@ -526,7 +527,7 @@
                 dma((chunks,)),
                 dma((chunks, n + 1)),
                 pltpu.SemaphoreType.REGULAR((chunks,)),
-                dma((n, 2)),
+                dma((2,)),
                 dma((PIECES, 2)),
                 dma((2, 3)),
                 dma((2, 2)),

time: 137 us -> 137 us (level)
  no operation moved by 1% of the time
where the time goes in v5:
time: 137 us
  Pallas kernels  136 us (99%)
    pallas_call x1, Pallas kernels, step(): pl.pallas_call(functools.partial(kernel, n), out_shape=(pltpu.VMEM((width...  125 us
    pallas_call x1, Pallas kernels, step(): pl.pallas_call(store, out_shape=[jax.ShapeDtypeStruct(a.shape, BF16) for...  10.9 us

profile of v5, /device:TPU:97, one launch (start us, length us, event | category | flops | bytes accessed | tf_op | source)
XLA Modules:
  0.0 137.0 jit_solution(14267981426694112926)
XLA Ops:
  0.6 125.5 %shard_map.102 = (bf16[5120,768]{1,0:T(8,128)(2,1)S(1)}, bf16[384,5120]{1,0:T(8,128)(2,1)S(1)}, bf16[1024,5120]{1,0:T(8,128)(2,1)S(1)}, bf16[1024,5120]{1,0:T(8,128)(2,1)S(1)}) custom-call(bf16[2048,5120]{1,0:T(8,128)(2,1)} %x.1, bf16[2048,5120]{1,0:T(8,128)(2,1)} %dy.1, bf16[2048,384]{1,0:T(8,128)(2,1)} %gate.1, bf16[2048,384]{1,0:T(8,128)(2,1)} %up.1, ...), custom_call_target="tpu_custom_call" | custom-call | tf_op jit(solution)/shard_map/pallas_call | solution.py:504
  126.1 10.9 %shard_map.103 = (bf16[2048,5120]{1,0:T(8,128)(2,1)}, bf16[5120,384]{1,0:T(8,128)(2,1)}, bf16[5120,384]{1,0:T(8,128)(2,1)}, bf16[384,5120]{1,0:T(8,128)(2,1)}) custom-call(bf16[5120,768]{1,0:T(8,128)(2,1)S(1)} %get-tuple-element.8.dw_gu, bf16[384,5120]{1,0:T(8,128)(2,1)S(1)} %get-tuple-element.9.dw_d, bf16[1024,5120]{1,0:T(8,128)(2,1)S(1)} %get-tuple-element.10.mine, ...), custom_call_target="tpu_custom_call" | custom-call | tf_op jit(solution)/shard_map/pallas_call | solution.py:539
